TPU v7x, 32 devices: a whole 2x2x4 slice. The times are simulated.
32 devices in a mesh: grp: 2 (over x), pool: 16 (over z, y, core).
Axes of the slice: x: 2, y: 2, z: 4, core: 2. Of those that a mesh axis runs over, the one named last changes fastest.
Arguments:
- query: bfloat16 [32, 4096], P(('grp', 'pool')), parts along dimension 0, may hold values from -6 to 6
- kv_pool: bfloat16 [2048, 2, 16, 512], P(('grp', 'pool')), parts along dimension 0, may hold values from -6 to 6
- holder_table: int32 [32, 128], P(('grp', 'pool')), parts along dimension 0, may hold values from 0 to 15, as said below
- slot_table: int32 [32, 128], P(('grp', 'pool')), parts along dimension 0, may hold values from 0 to 63
- lengths: int32 [32], P(('grp', 'pool')), parts along dimension 0, may hold values from 96 to 128, as said below
- out_weight: bfloat16 [4096, 8192], P('pool'), may hold values from -1.1953125 to 1.1953125
Outputs:
- mixed: bfloat16 [32, 8192], P(('grp', 'pool')), parts along dimension 0
There are 2 independent parts, one for each index of `grp`. A program takes and returns all parts, laid end to end along the dimension named above; an argument that names none is the same for every part. Nothing has to cross between parts.
Inputs may be any that keep to these rules, and one draw needn't show every extreme that they name: `holder_table`: entry [r, j] is the index along pool of the device holding block j of request r. Of one request's 128 blocks at most 16 have the same holder, and some holder has exactly 16 of the request's first 96 blocks. Request r's live blocks are 0 to lengths[r] - 1; some request has 128.
All inputs are finite; a program needn't handle non-finite values.
Results may differ from a plain program's by a relative error of at most 0.0053.
Values may be sent and summed in bfloat16 or wider, within the bound.
A program may use at most 64 MiB of HBM per device.

v0:
```python
import math
import jax
import jax.numpy as jnp
from jax import lax
from jax.sharding import PartitionSpec as P

H = 32
KVH = 4
HD = 128
lowest = -1e30


def block_partials(query_heads, kv_blocks):
    head_dim = query_heads.shape[-1]
    kv_heads = query_heads.shape[1]
    block_len = kv_blocks.shape[3]
    block_shape = kv_blocks.shape[:2] + (block_len, kv_heads, head_dim)
    key_part = kv_blocks[:, :, 0].reshape(block_shape)
    value_part = kv_blocks[:, :, 1].reshape(block_shape)
    scores = jnp.einsum(
        "agqd,acbgd->acgqb", query_heads, key_part, preferred_element_type=jnp.float32
    )
    scores = scores * (1.0 / math.sqrt(head_dim))
    maxima = jnp.max(scores, axis=-1)
    shifted = jnp.exp(scores - maxima[..., None])
    totals = jnp.sum(shifted, axis=-1)
    outputs = jnp.einsum(
        "acgqb,acbgd->acgqd",
        shifted.astype(jnp.bfloat16),
        value_part,
        preferred_element_type=jnp.float32,
    )
    return (maxima, outputs, totals)


def merge_blocks(maxima, outputs, totals, live_mask, axis_pos):
    peak_score = jnp.max(jnp.where(live_mask, maxima, lowest), axis=axis_pos, keepdims=True)
    factor = jnp.exp(jnp.where(live_mask, maxima - peak_score, lowest))
    numerator = jnp.sum(factor[..., None] * outputs, axis=axis_pos)
    denominator = jnp.sum(factor * totals, axis=axis_pos)
    return (jnp.squeeze(peak_score, axis_pos), numerator, denominator)


def per_device(query, kv_pool, holder_table, slot_table, lengths, out_weight):
    pool_size = lax.axis_size("pool")
    my_index = lax.axis_index("pool")
    max_blocks = holder_table.shape[1]
    capacity = 2 * max_blocks // pool_size
    groups = H // KVH
    all_holders, all_slots, all_lengths = (
        lax.all_gather(holder_table, "pool", axis=0, tiled=True),
        lax.all_gather(slot_table, "pool", axis=0, tiled=True),
        lax.all_gather(lengths, "pool", axis=0, tiled=True),
    )
    cap_iota = jnp.arange(capacity, dtype=jnp.int32)
    block_iota = jnp.arange(max_blocks, dtype=jnp.int32)
    held_here = all_holders == my_index
    rank_here = jnp.cumsum(held_here.astype(jnp.int32), axis=1) - 1
    pick_hot = held_here[:, None, :] & (rank_here[:, None, :] == cap_iota[None, :, None])
    pick_slot = jnp.sum(jnp.where(pick_hot, all_slots[:, None, :], 0), axis=-1)
    pick_block = jnp.sum(jnp.where(pick_hot, block_iota[None, None, :], 0), axis=-1)
    send_live = jnp.any(pick_hot, axis=-1) & (pick_block < all_lengths[:, None])
    send_blocks = kv_pool[pick_slot]
    all_queries = lax.all_gather(query, "pool", axis=0, tiled=True)
    maxima, outputs, totals = block_partials(
        all_queries.reshape(pool_size, KVH, groups, HD), send_blocks
    )
    part_peak, part_numer, part_denom = merge_blocks(
        maxima, outputs, totals, send_live[:, :, None, None], 1
    )
    got_peak, got_numer, got_denom = (
        lax.all_to_all(
            part_peak.reshape(pool_size, H), "pool", split_axis=0, concat_axis=0, tiled=True
        ),
        lax.all_to_all(
            part_numer.reshape(pool_size, H * HD), "pool", split_axis=0, concat_axis=0, tiled=True
        ),
        lax.all_to_all(
            part_denom.reshape(pool_size, H), "pool", split_axis=0, concat_axis=0, tiled=True
        ),
    )
    peak_score, numerator, denominator = merge_blocks(
        got_peak.reshape(pool_size, KVH, groups),
        got_numer.reshape(pool_size, KVH, groups, HD),
        got_denom.reshape(pool_size, KVH, groups),
        True,
        0,
    )
    attention = (numerator / denominator[..., None]).reshape(1, H * HD).astype(jnp.bfloat16)
    features = lax.all_to_all(attention, "pool", split_axis=1, concat_axis=0, tiled=True)
    return lax.psum_scatter(
        jnp.dot(features, out_weight, preferred_element_type=jnp.float32),
        "pool",
        scatter_dimension=0,
        tiled=True,
    ).astype(jnp.bfloat16)


def solution(mesh):
    placed = (
        P(("grp", "pool"), None),
        P(("grp", "pool"), None, None, None),
        P(("grp", "pool"), None),
        P(("grp", "pool"), None),
        P(("grp", "pool")),
        P("pool", None),
    )
    return jax.shard_map(
        per_device, mesh=mesh, in_specs=placed, out_specs=P(("grp", "pool"), None), check_vma=False
    )
```

profile of v0, /device:TPU:0, one launch (start us, length us, event | category | flops | bytes accessed | tf_op | source)
XLA Modules:
  0.0 231.0 jit_solution(6533422985778512869)
XLA Ops:
  0.0 23.4 %all-gather = s32[16,1,128]{2,1,0:T(1,128)S(1)} all-gather(s32[1,1,128]{2,1,0:T(1,128)} %bitcast.78), channel_id=1, replica_groups=mesh['grp'=2,'pool'=16] {'pool'}, dimensions={0}, use_global_device_ids=true | all-gather | bytes 8704 | tf_op jit(solution)/shard_map/all_gather | solution.py:51
  23.7 17.6 %all-gather.1 = s32[16,1,128]{2,1,0:T(1,128)S(1)} all-gather(s32[1,1,128]{2,1,0:T(1,128)} %bitcast.79), channel_id=1, replica_groups=mesh['grp'=2,'pool'=16] {'pool'}, dimensions={0}, use_global_device_ids=true | all-gather | bytes 8704 | tf_op jit(solution)/shard_map/all_gather | solution.py:52
  42.6 1.3 fusion.18
  43.9 0.8 dynamic-update-slice
  45.0 9.4 %all-reduce = s32[16]{0:T(128)S(1)} all-reduce(s32[16]{0:T(128)S(1)} %dynamic-update-slice), channel_id=1, replica_groups=mesh['grp'=2,'pool'=16] {'pool'}, use_global_device_ids=true, to_apply=%add | all-reduce | flops 16 | bytes 128
  54.5 8.5 %gather_fusion = bf16[256,2,16,512]{3,2,1,0:T(8,128)(2,1)} fusion(bf16[64,2,16,512]{3,2,1,0:T(8,128)(2,1)S(1)} %copy-done, s32[1024]{0:T(1024)S(1)} %pad_clamp_fusion), kind=kCustom, calls=%fused_computation | custom fusion | bytes 16778240 | tf_op jit(solution)/shard_map/gather | solution.py:63
  63.0 6.1 %slice_bitcast_fusion = (bf16[16,16,1,16,512]{4,3,1,0,2:T(8,128)(2,1)}, bf16[16,16,1,16,512]{4,3,1,0,2:T(8,128)(2,1)}) fusion(bf16[16,16,2,16,512]{4,3,2,1,0:T(8,128)(2,1)} %bitcast.64), kind=kLoop, calls=%fused_computation.1 | loop fusion | bytes 16777216
  69.1 6.9 %reshape_squeeze.6 = bf16[16,16,16,4,128]{4,3,2,1,0:T(4,128)(2,1)} reshape(bf16[16,16,1,16,512]{4,3,1,0,2:T(8,128)(2,1)} %get-tuple-element.12) | data formatting | bytes 8388608 | tf_op jit(solution)/shard_map/reshape;squeeze | solution.py:18
  76.0 21.5 %all-gather.2 = bf16[16,1,4096]{2,1,0:T(2,128)(2,1)S(1)} all-gather(bf16[1,1,4096]{2,1,0:T(2,128)(2,1)S(1)} %bitcast.77), channel_id=1, replica_groups=mesh['grp'=2,'pool'=16] {'pool'}, dimensions={0}, use_global_device_ids=true | all-gather | bytes 139264 | tf_op jit(solution)/shard_map/all_gather | solution.py:64
  97.5 0.7 reduce.6
  98.3 12.2 %bitcast_reduce_fusion = (f32[16,16,4,8]{3,1,2,0:T(8,128)S(1)}, f32[16,4,16,16,8]{3,4,2,1,0:T(8,128)S(1)}) fusion(bf16[16,4,8,128,1]{3,2,1,0,4:T(8,128)(2,1)S(1)} %bitcast.66, bf16[16,16,16,4,128]{4,3,2,1,0:T(4,128)(2,1)} %reshape_squeeze.6), kind=kOutput, calls=%fused_computation.4 | convolution fusion | flops 33808384 | bytes 4882432 | tf_op jit(solution)/shard_map/agqd,acbgd->acgqb/dot_general | solution.py:20
  110.7 2.9 %fusion.5 = (f32[16,16,4,8]{3,1,2,0:T(8,128)S(1)}, bf16[16,16,4,8,16]{4,3,1,2,0:T(8,128)(2,1)}) fusion(f32[16,4,16,16,8]{3,4,2,1,0:T(8,128)S(1)} %get-tuple-element.18, f32[16,16,4,8]{3,1,2,0:T(8,128)S(1)} %get-tuple-element.17), kind=kLoop, calls=%fused_computation.11 | loop fusion | flops 516096 | bytes 851968 | tf_op jit(solution)/shard_map/reduce_sum | solution.py:26
  114.7 3.4 %all-to-all-start.2 = ((f32[16,1,32]{2,1,0:T(1,128)}), f32[16,1,32]{2,1,0:T(1,128)S(1)}, u32[]{:S(2)}, u32[]{:S(2)}) async-start(f32[16,1,32]{2,1,0:T(1,128)} %copy.55), calls=%async_computation.2 | async-start | bytes 16384 | tf_op jit(solution)/shard_map/all_to_all | solution.py:78
  119.1 6.9 %reshape_squeeze.7 = bf16[16,16,16,4,128]{4,3,2,1,0:T(4,128)(2,1)} reshape(bf16[16,16,1,16,512]{4,3,1,0,2:T(8,128)(2,1)} %get-tuple-element.11) | data formatting | bytes 8388608 | tf_op jit(solution)/shard_map/reshape;squeeze | solution.py:19
  126.0 6.0 %all-to-all-start = ((f32[16,1,32]{2,1,0:T(1,128)}), f32[16,1,32]{2,1,0:T(1,128)S(1)}, u32[]{:S(2)}, u32[]{:S(2)}) async-start(f32[16,1,32]{2,1,0:T(1,128)} %copy.47), calls=%async_computation | async-start | bytes 16384 | tf_op jit(solution)/shard_map/all_to_all | solution.py:72
  132.0 5.0 %multiply_reduce_fusion = f32[16,4,8,128]{3,2,1,0:T(8,128)} fusion(bf16[16,16,16,4,128]{4,3,2,1,0:T(4,128)(2,1)} %reshape_squeeze.7, bf16[16,16,4,8,16]{4,3,1,2,0:T(8,128)(2,1)} %get-tuple-element.14, f32[16,16,4,8]{3,2,1,0:T(4,128)S(1)} %copy.50), kind=kOutput, calls=%fused_computation.10 | convolution fusion | flops 35586048 | bytes 4751360 | tf_op jit(solution)/shard_map/acgqb,acbgd->acgqd/dot_general | solution.py:27
  137.0 1.3 all-to-all-done
  138.3 4.7 %all-to-all-start.1 = ((f32[16,1,4096]{2,1,0:T(1,128)}), f32[16,1,4096]{2,1,0:T(1,128)S(1)}, u32[]{:S(2)}, u32[]{:S(2)}) async-start(f32[16,1,4096]{2,1,0:T(1,128)} %bitcast.14), calls=%async_computation.1 | async-start | bytes 524288 | tf_op jit(solution)/shard_map/all_to_all | solution.py:75
  143.5 9.5 %all-to-all-done.1 = f32[16,1,4096]{2,1,0:T(1,128)S(1)} async-done(((f32[16,1,4096]{2,1,0:T(1,128)}), f32[16,1,4096]{2,1,0:T(1,128)S(1)}, u32[]{:S(2)}, u32[]{:S(2)}) %all-to-all-start.1) | async-done | bytes 262176 | tf_op jit(solution)/shard_map/all_to_all | solution.py:75
  154.1 0.7 reduce.7
  154.8 9.1 %all_to_all.46 = bf16[16,2,128]{2,1,0:T(2,128)(2,1)S(1)} all-to-all(bf16[16,2,128]{2,1,0:T(2,128)(2,1)S(1)} %reshape.157), channel_id=1, replica_groups=mesh['grp'=2,'pool'=16] {'pool'}, dimensions={0} | all-to-all | bytes 16384 | tf_op jit(solution)/shard_map/all_to_all | solution.py:90
  163.9 2.8 %fusion.14 = f32[16,8192]{1,0:T(8,128)S(1)} fusion(bf16[256,8192]{1,0:T(8,128)(2,1)} %param.11, bf16[1,16,256]{2,0,1:T(2,128)(2,1)S(1)} %bitcast.73), kind=kOutput, calls=%fused_computation.29 | convolution fusion | flops 67108864 | bytes 4726784 | tf_op jit(solution)/shard_map/dot_general | solution.py:92
  166.8 63.0 %all-reduce.3 = bf16[16,8192]{1,0:T(8,128)(2,1)S(1)} all-reduce(f32[16,8192]{1,0:T(8,128)S(1)} %fusion.14), channel_id=2, replica_groups=mesh['grp'=2,'pool'=16] {'pool'}, use_global_device_ids=true, to_apply=%region_12.13.clone | all-reduce | flops 131072 | bytes 786432
  229.8 1.2 dynamic-slice_convert_fusion
  (37 shorter events, 5.2 us)
Async XLA Ops:
  0.0 54.5 %copy-start = (bf16[64,2,16,512]{3,2,1,0:T(8,128)(2,1)S(1)}, bf16[64,2,16,512]{3,2,1,0:T(8,128)(2,1)}, u32[]{:S(2)}) copy-start(bf16[64,2,16,512]{3,2,1,0:T(8,128)(2,1)} %param.7) | copy-start | bytes 6291460
  69.1 6.9 %copy-start.1 = (bf16[1,4096]{1,0:T(2,128)(2,1)S(1)}, bf16[1,4096]{1,0:T(2,128)(2,1)}, u32[]{:S(2)}) copy-start(bf16[1,4096]{1,0:T(2,128)(2,1)} %param.6) | copy-start | bytes 24580
  114.7 11.3 %all-to-all-start.2 = ((f32[16,1,32]{2,1,0:T(1,128)}), f32[16,1,32]{2,1,0:T(1,128)S(1)}, u32[]{:S(2)}, u32[]{:S(2)}) async-start(f32[16,1,32]{2,1,0:T(1,128)} %copy.55), calls=%async_computation.2 | async-start | bytes 16384 | tf_op jit(solution)/shard_map/all_to_all | solution.py:78
  126.0 12.3 %all-to-all-start = ((f32[16,1,32]{2,1,0:T(1,128)}), f32[16,1,32]{2,1,0:T(1,128)S(1)}, u32[]{:S(2)}, u32[]{:S(2)}) async-start(f32[16,1,32]{2,1,0:T(1,128)} %copy.47), calls=%async_computation | async-start | bytes 16384 | tf_op jit(solution)/shard_map/all_to_all | solution.py:72
  138.3 14.7 %all-to-all-start.1 = ((f32[16,1,4096]{2,1,0:T(1,128)}), f32[16,1,4096]{2,1,0:T(1,128)S(1)}, u32[]{:S(2)}, u32[]{:S(2)}) async-start(f32[16,1,4096]{2,1,0:T(1,128)} %bitcast.14), calls=%async_computation.1 | async-start | bytes 524288 | tf_op jit(solution)/shard_map/all_to_all | solution.py:75
where the time goes:
time: 232 us; the launch traced here: 231 us
  blocking collectives  144 us (62%)
  local copies, waits for them, and re-layouts  34.6 us (15%)
  matrix products  20 us (9%)
  starting transfers between devices  14.1 us (6%)
  waiting for transfers between devices  10.9 us (5%)
  other arithmetic  6.65 us (3%)
    unnamed x2, blocking collectives  72.4 us
    all_gather x1, blocking collectives, per_device(): lax.all_gather(holder_table, 'pool', axis=0, tiled=True)  23.4 us
    all_gather x1, blocking collectives, per_device(): all_queries = lax.all_gather(query, 'pool', axis=0, tiled=True)  21.5 us
    all_gather x1, blocking collectives, per_device(): lax.all_gather(slot_table, 'pool', axis=0, tiled=True)  17.6 us
    dot_general x1, matrix products, block_partials(): jnp.einsum('agqd,acbgd->acgqb', query_heads, key_part, preferred_element_...  12.2 us
    all_to_all x1, waiting for transfers between devices, per_device(): lax.all_to_all(part_numer.reshape(pool_size, H * HD), 'pool', split_axis=...  9.54 us
    all_to_all x1, blocking collectives, per_device(): lax.all_to_all(attention, 'pool', split_axis=1, concat_axis=0, tiled=True)  9.11 us
    unnamed x12, local copies, waits for them, and re-layouts  8.72 us
  transfers between devices with their start and end apart: 3, of which 2 were waited for; matrix products, arithmetic and copies ran while one was open for 6% of the time, Pallas kernels for 0%

commit v1 on v0

--- a/solution.py
+++ b/solution.py
@@ -61,7 +61,14 @@
     pick_block = jnp.sum(jnp.where(pick_hot, block_iota[None, None, :], 0), axis=-1)
     send_live = jnp.any(pick_hot, axis=-1) & (pick_block < all_lengths[:, None])
     send_blocks = kv_pool[pick_slot]
-    all_queries = lax.all_gather(query, "pool", axis=0, tiled=True)
+    size = lax.axis_size("pool")
+    hops = [(i, (i + 1) % size) for i in range(size)]
+    terms = [query]
+    for hop in range(1, size):
+        terms = [lax.ppermute(terms[0], "pool", hops), *terms]
+    full = jnp.concatenate(terms, axis=0)
+    offset = (lax.axis_index("pool") + 1) * terms[-1].shape[0]
+    all_queries = jnp.roll(full, offset, axis=0)
     maxima, outputs, totals = block_partials(
         all_queries.reshape(pool_size, KVH, groups, HD), send_blocks
     )

time: 232 us -> 264 us (1.14)
  waiting for transfers between devices: 10.9 us -> 63 us
  blocking collectives: 144 us -> 121 us
  starting transfers between devices: 14.1 us -> 17.4 us
    ppermute x0 -> x15, waiting for transfers between devices: none -> 52.2 us  [per_device(): terms = [lax.ppermute(terms[0], 'pool', hops), *terms]]
    all_gather x1 -> x0, blocking collectives: 21.5 us -> none  [per_device(): all_queries = lax.all_gather(query, 'pool', axis=0, tiled=True)]
    all_gather x1, blocking collectives: 23.4 us -> 18.2 us  [per_device(): lax.all_gather(holder_table, 'pool', axis=0, tiled=True)]
    unnamed x2, blocking collectives: 72.4 us -> 75.5 us
    unnamed x12 -> x15, local copies, waits for them, and re-layouts: 8.72 us -> 8.07 us
  transfers between devices with their start and end apart: 3 -> 18, of which waited for: 2 -> 11; matrix products, arithmetic and copies ran while one was open for 6% -> 14% of each run, Pallas kernels for 0% -> 0%
where the time goes in v1:
time: 264 us; the launch traced here: 263 us
  blocking collectives  121 us (46%)
  waiting for transfers between devices  63 us (24%)
  local copies, waits for them, and re-layouts  34.8 us (13%)
  matrix products  20 us (8%)
  starting transfers between devices  17.4 us (7%)
  other arithmetic  5.91 us (2%)
    unnamed x2, blocking collectives  75.5 us
    ppermute x15, waiting for transfers between devices, per_device(): terms = [lax.ppermute(terms[0], 'pool', hops), *terms]  52.2 us
    all_gather x1, blocking collectives, per_device(): lax.all_gather(holder_table, 'pool', axis=0, tiled=True)  18.2 us
    all_gather x1, blocking collectives, per_device(): lax.all_gather(slot_table, 'pool', axis=0, tiled=True)  18.2 us
    dot_general x1, matrix products, block_partials(): jnp.einsum('agqd,acbgd->acgqb', query_heads, key_part, preferred_element_...  12.2 us
    all_to_all x1, waiting for transfers between devices, per_device(): lax.all_to_all(part_numer.reshape(pool_size, H * HD), 'pool', split_axis=...  9.54 us
    all_to_all x1, blocking collectives, per_device(): lax.all_to_all(attention, 'pool', split_axis=1, concat_axis=0, tiled=True)  9.11 us
    gather x1, local copies, waits for them, and re-layouts, per_device(): send_blocks = kv_pool[pick_slot]  8.47 us
  transfers between devices with their start and end apart: 18, of which 11 were waited for; matrix products, arithmetic and copies ran while one was open for 14% of the time, Pallas kernels for 0%

profile of v1, /device:TPU:0, one launch (start us, length us, event | category | flops | bytes accessed | tf_op | source)
XLA Modules:
  0.0 263.0 jit_solution(13171096648786176837)
XLA Ops:
  0.5 6.6 %collective-permute-done = bf16[1,4096]{1,0:T(2,128)(2,1)S(1)} collective-permute-done((bf16[1,4096]{1,0:T(2,128)(2,1)}, bf16[1,4096]{1,0:T(2,128)(2,1)S(1)}, u32[]{:S(2)}, u32[]{:S(2)}) %collective-permute-start) | collective-permute-done | bytes 8224 | tf_op jit(solution)/shard_map/ppermute | solution.py:68
  7.1 5.9 %collective-permute-done.1 = bf16[1,4096]{1,0:T(2,128)(2,1)S(1)} collective-permute-done((bf16[1,4096]{1,0:T(2,128)(2,1)S(1)}, bf16[1,4096]{1,0:T(2,128)(2,1)S(1)}, u32[]{:S(2)}, u32[]{:S(2)}) %collective-permute-start.1) | collective-permute-done | bytes 8224 | tf_op jit(solution)/shard_map/ppermute | solution.py:68
  13.0 5.9 %collective-permute-done.2 = bf16[1,4096]{1,0:T(2,128)(2,1)S(1)} collective-permute-done((bf16[1,4096]{1,0:T(2,128)(2,1)S(1)}, bf16[1,4096]{1,0:T(2,128)(2,1)S(1)}, u32[]{:S(2)}, u32[]{:S(2)}) %collective-permute-start.2) | collective-permute-done | bytes 8224 | tf_op jit(solution)/shard_map/ppermute | solution.py:68
  18.8 5.9 %collective-permute-done.3 = bf16[1,4096]{1,0:T(2,128)(2,1)S(1)} collective-permute-done((bf16[1,4096]{1,0:T(2,128)(2,1)S(1)}, bf16[1,4096]{1,0:T(2,128)(2,1)S(1)}, u32[]{:S(2)}, u32[]{:S(2)}) %collective-permute-start.3) | collective-permute-done | bytes 8224 | tf_op jit(solution)/shard_map/ppermute | solution.py:68
  24.7 5.9 %collective-permute-done.4 = bf16[1,4096]{1,0:T(2,128)(2,1)S(1)} collective-permute-done((bf16[1,4096]{1,0:T(2,128)(2,1)S(1)}, bf16[1,4096]{1,0:T(2,128)(2,1)S(1)}, u32[]{:S(2)}, u32[]{:S(2)}) %collective-permute-start.4) | collective-permute-done | bytes 8224 | tf_op jit(solution)/shard_map/ppermute | solution.py:68
  30.6 5.9 %collective-permute-done.5 = bf16[1,4096]{1,0:T(2,128)(2,1)S(1)} collective-permute-done((bf16[1,4096]{1,0:T(2,128)(2,1)S(1)}, bf16[1,4096]{1,0:T(2,128)(2,1)S(1)}, u32[]{:S(2)}, u32[]{:S(2)}) %collective-permute-start.5) | collective-permute-done | bytes 8224 | tf_op jit(solution)/shard_map/ppermute | solution.py:68
  36.4 18.2 %all-gather = s32[16,1,128]{2,1,0:T(1,128)S(1)} all-gather(s32[1,1,128]{2,1,0:T(1,128)} %bitcast.76), channel_id=1, replica_groups=mesh['grp'=2,'pool'=16] {'pool'}, dimensions={0}, use_global_device_ids=true | all-gather | bytes 8704 | tf_op jit(solution)/shard_map/all_gather | solution.py:51
  55.0 5.4 %collective-permute-done.7 = bf16[1,4096]{1,0:T(2,128)(2,1)S(1)} collective-permute-done((bf16[1,4096]{1,0:T(2,128)(2,1)S(1)}, bf16[1,4096]{1,0:T(2,128)(2,1)S(1)}, u32[]{:S(2)}, u32[]{:S(2)}) %collective-permute-start.7) | collective-permute-done | bytes 8224 | tf_op jit(solution)/shard_map/ppermute | solution.py:68
  60.5 18.2 %all-gather.1 = s32[16,1,128]{2,1,0:T(1,128)S(1)} all-gather(s32[1,1,128]{2,1,0:T(1,128)} %bitcast.77), channel_id=1, replica_groups=mesh['grp'=2,'pool'=16] {'pool'}, dimensions={0}, use_global_device_ids=true | all-gather | bytes 8704 | tf_op jit(solution)/shard_map/all_gather | solution.py:52
  79.4 5.1 %collective-permute-done.9 = bf16[1,4096]{1,0:T(2,128)(2,1)S(1)} collective-permute-done((bf16[1,4096]{1,0:T(2,128)(2,1)S(1)}, bf16[1,4096]{1,0:T(2,128)(2,1)S(1)}, u32[]{:S(2)}, u32[]{:S(2)}) %collective-permute-start.9) | collective-permute-done | bytes 8224 | tf_op jit(solution)/shard_map/ppermute | solution.py:68
  84.6 5.8 %collective-permute-done.10 = bf16[1,4096]{1,0:T(2,128)(2,1)S(1)} collective-permute-done((bf16[1,4096]{1,0:T(2,128)(2,1)S(1)}, bf16[1,4096]{1,0:T(2,128)(2,1)S(1)}, u32[]{:S(2)}, u32[]{:S(2)}) %collective-permute-start.10) | collective-permute-done | bytes 8224 | tf_op jit(solution)/shard_map/ppermute | solution.py:68
  90.4 8.5 %gather_fusion = bf16[256,2,16,512]{3,2,1,0:T(8,128)(2,1)} fusion(bf16[64,2,16,512]{3,2,1,0:T(8,128)(2,1)S(1)} %copy-done, s32[1024]{0:T(1024)S(1)} %pad_clamp_fusion), kind=kCustom, calls=%fused_computation | custom fusion | bytes 16778240 | tf_op jit(solution)/shard_map/gather | solution.py:63
  98.8 6.1 %slice_bitcast_fusion = (bf16[16,16,1,16,512]{4,3,1,0,2:T(8,128)(2,1)}, bf16[16,16,1,16,512]{4,3,1,0,2:T(8,128)(2,1)}) fusion(bf16[16,16,2,16,512]{4,3,2,1,0:T(8,128)(2,1)} %bitcast.64), kind=kLoop, calls=%fused_computation.1 | loop fusion | bytes 16777216
  107.3 12.6 %all-reduce = s32[16]{0:T(128)S(1)} all-reduce(s32[16]{0:T(128)S(1)} %dynamic-update-slice), channel_id=1, replica_groups=mesh['grp'=2,'pool'=16] {'pool'}, use_global_device_ids=true, to_apply=%add | all-reduce | flops 16 | bytes 128
  120.0 6.9 %reshape_squeeze.6 = bf16[16,16,16,4,128]{4,3,2,1,0:T(4,128)(2,1)} reshape(bf16[16,16,1,16,512]{4,3,1,0,2:T(8,128)(2,1)} %get-tuple-element.12) | data formatting | bytes 8388608 | tf_op jit(solution)/shard_map/reshape;squeeze | solution.py:18
  127.8 12.2 %bitcast_reduce_fusion = (f32[16,16,4,8]{3,1,2,0:T(8,128)S(1)}, f32[16,4,16,16,8]{3,4,2,1,0:T(8,128)S(1)}) fusion(bf16[16,4,8,128,1]{3,2,1,0,4:T(8,128)(2,1)S(1)} %bitcast.66, bf16[16,16,16,4,128]{4,3,2,1,0:T(4,128)(2,1)} %reshape_squeeze.6), kind=kOutput, calls=%fused_computation.4 | convolution fusion | flops 33808384 | bytes 4882432 | tf_op jit(solution)/shard_map/agqd,acbgd->acgqb/dot_general | solution.py:20
  144.1 5.8 %all-to-all-start.2 = ((f32[16,1,32]{2,1,0:T(1,128)}), f32[16,1,32]{2,1,0:T(1,128)S(1)}, u32[]{:S(2)}, u32[]{:S(2)}) async-start(f32[16,1,32]{2,1,0:T(1,128)} %copy.55), calls=%async_computation.2 | async-start | bytes 16384 | tf_op jit(solution)/shard_map/all_to_all | solution.py:85
  150.0 6.9 %reshape_squeeze.7 = bf16[16,16,16,4,128]{4,3,2,1,0:T(4,128)(2,1)} reshape(bf16[16,16,1,16,512]{4,3,1,0,2:T(8,128)(2,1)} %get-tuple-element.11) | data formatting | bytes 8388608 | tf_op jit(solution)/shard_map/reshape;squeeze | solution.py:19
  157.9 6.0 %all-to-all-start = ((f32[16,1,32]{2,1,0:T(1,128)}), f32[16,1,32]{2,1,0:T(1,128)S(1)}, u32[]{:S(2)}, u32[]{:S(2)}) async-start(f32[16,1,32]{2,1,0:T(1,128)} %copy.47), calls=%async_computation | async-start | bytes 16384 | tf_op jit(solution)/shard_map/all_to_all | solution.py:79
  163.9 5.0 %multiply_reduce_fusion = f32[16,4,8,128]{3,2,1,0:T(8,128)} fusion(bf16[16,16,16,4,128]{4,3,2,1,0:T(4,128)(2,1)} %reshape_squeeze.7, bf16[16,16,4,8,16]{4,3,1,2,0:T(8,128)(2,1)} %get-tuple-element.14, f32[16,16,4,8]{3,2,1,0:T(4,128)S(1)} %copy.50), kind=kOutput, calls=%fused_computation.10 | convolution fusion | flops 35586048 | bytes 4751360 | tf_op jit(solution)/shard_map/acgqb,acbgd->acgqd/dot_general | solution.py:27
  170.2 4.7 %all-to-all-start.1 = ((f32[16,1,4096]{2,1,0:T(1,128)}), f32[16,1,4096]{2,1,0:T(1,128)S(1)}, u32[]{:S(2)}, u32[]{:S(2)}) async-start(f32[16,1,4096]{2,1,0:T(1,128)} %bitcast.13), calls=%async_computation.1 | async-start | bytes 524288 | tf_op jit(solution)/shard_map/all_to_all | solution.py:82
  175.4 9.5 %all-to-all-done.1 = f32[16,1,4096]{2,1,0:T(1,128)S(1)} async-done(((f32[16,1,4096]{2,1,0:T(1,128)}), f32[16,1,4096]{2,1,0:T(1,128)S(1)}, u32[]{:S(2)}, u32[]{:S(2)}) %all-to-all-start.1) | async-done | bytes 262176 | tf_op jit(solution)/shard_map/all_to_all | solution.py:82
  186.7 9.1 %all_to_all.46 = bf16[16,2,128]{2,1,0:T(2,128)(2,1)S(1)} all-to-all(bf16[16,2,128]{2,1,0:T(2,128)(2,1)S(1)} %reshape.153), channel_id=1, replica_groups=mesh['grp'=2,'pool'=16] {'pool'}, dimensions={0} | all-to-all | bytes 16384 | tf_op jit(solution)/shard_map/all_to_all | solution.py:97
  198.7 63.0 %all-reduce.3 = bf16[16,8192]{1,0:T(8,128)(2,1)S(1)} all-reduce(f32[16,8192]{1,0:T(8,128)S(1)} %fusion.14), channel_id=2, replica_groups=mesh['grp'=2,'pool'=16] {'pool'}, use_global_device_ids=true, to_apply=%region_12.13.clone | all-reduce | flops 131072 | bytes 786432
  (69 shorter events, 17.4 us)
Async XLA Ops:
  0.0 90.4 %copy-start = (bf16[64,2,16,512]{3,2,1,0:T(8,128)(2,1)S(1)}, bf16[64,2,16,512]{3,2,1,0:T(8,128)(2,1)}, u32[]{:S(2)}) copy-start(bf16[64,2,16,512]{3,2,1,0:T(8,128)(2,1)} %param.7) | copy-start | bytes 6291460
  0.0 7.1 %collective-permute-start = (bf16[1,4096]{1,0:T(2,128)(2,1)}, bf16[1,4096]{1,0:T(2,128)(2,1)S(1)}, u32[]{:S(2)}, u32[]{:S(2)}) collective-permute-start(bf16[1,4096]{1,0:T(2,128)(2,1)} %param.6), channel_id=1, source_target_pairs={{0,1},{1,2},{2,3},{3,4},{4,5},{5,6},{6,7},{7,8},{8,9},{9,10},{10,1... | collective-permute-start | bytes 24584 | tf_op jit(solution)/shard_map/ppermute | solution.py:68
  7.1 5.9 %collective-permute-start.1 = (bf16[1,4096]{1,0:T(2,128)(2,1)S(1)}, bf16[1,4096]{1,0:T(2,128)(2,1)S(1)}, u32[]{:S(2)}, u32[]{:S(2)}) collective-permute-start(bf16[1,4096]{1,0:T(2,128)(2,1)S(1)} %collective-permute-done), channel_id=1, source_target_pairs={{0,1},{1,2},{2,3},{3,4},{4,5},{5,6},{6,7},{7,8},{8,9},{9,10},{10,1... | collective-permute-start | bytes 24584 | tf_op jit(solution)/shard_map/ppermute | solution.py:68
  13.0 5.9 %collective-permute-start.2 = (bf16[1,4096]{1,0:T(2,128)(2,1)S(1)}, bf16[1,4096]{1,0:T(2,128)(2,1)S(1)}, u32[]{:S(2)}, u32[]{:S(2)}) collective-permute-start(bf16[1,4096]{1,0:T(2,128)(2,1)S(1)} %collective-permute-done.1), channel_id=1, source_target_pairs={{0,1},{1,2},{2,3},{3,4},{4,5},{5,6},{6,7},{7,8},{8,9},{9,10},{10,1... | collective-permute-start | bytes 24584 | tf_op jit(solution)/shard_map/ppermute | solution.py:68
  18.8 5.9 %collective-permute-start.3 = (bf16[1,4096]{1,0:T(2,128)(2,1)S(1)}, bf16[1,4096]{1,0:T(2,128)(2,1)S(1)}, u32[]{:S(2)}, u32[]{:S(2)}) collective-permute-start(bf16[1,4096]{1,0:T(2,128)(2,1)S(1)} %collective-permute-done.2), channel_id=1, source_target_pairs={{0,1},{1,2},{2,3},{3,4},{4,5},{5,6},{6,7},{7,8},{8,9},{9,10},{10,1... | collective-permute-start | bytes 24584 | tf_op jit(solution)/shard_map/ppermute | solution.py:68
  24.7 5.9 %collective-permute-start.4 = (bf16[1,4096]{1,0:T(2,128)(2,1)S(1)}, bf16[1,4096]{1,0:T(2,128)(2,1)S(1)}, u32[]{:S(2)}, u32[]{:S(2)}) collective-permute-start(bf16[1,4096]{1,0:T(2,128)(2,1)S(1)} %collective-permute-done.3), channel_id=1, source_target_pairs={{0,1},{1,2},{2,3},{3,4},{4,5},{5,6},{6,7},{7,8},{8,9},{9,10},{10,1... | collective-permute-start | bytes 24584 | tf_op jit(solution)/shard_map/ppermute | solution.py:68
  30.6 5.9 %collective-permute-start.5 = (bf16[1,4096]{1,0:T(2,128)(2,1)S(1)}, bf16[1,4096]{1,0:T(2,128)(2,1)S(1)}, u32[]{:S(2)}, u32[]{:S(2)}) collective-permute-start(bf16[1,4096]{1,0:T(2,128)(2,1)S(1)} %collective-permute-done.4), channel_id=1, source_target_pairs={{0,1},{1,2},{2,3},{3,4},{4,5},{5,6},{6,7},{7,8},{8,9},{9,10},{10,1... | collective-permute-start | bytes 24584 | tf_op jit(solution)/shard_map/ppermute | solution.py:68
  36.4 18.2 %collective-permute-start.6 = (bf16[1,4096]{1,0:T(2,128)(2,1)S(1)}, bf16[1,4096]{1,0:T(2,128)(2,1)S(1)}, u32[]{:S(2)}, u32[]{:S(2)}) collective-permute-start(bf16[1,4096]{1,0:T(2,128)(2,1)S(1)} %collective-permute-done.5), channel_id=1, source_target_pairs={{0,1},{1,2},{2,3},{3,4},{4,5},{5,6},{6,7},{7,8},{8,9},{9,10},{10,1... | collective-permute-start | bytes 24584 | tf_op jit(solution)/shard_map/ppermute | solution.py:68
  54.6 5.9 %collective-permute-start.7 = (bf16[1,4096]{1,0:T(2,128)(2,1)S(1)}, bf16[1,4096]{1,0:T(2,128)(2,1)S(1)}, u32[]{:S(2)}, u32[]{:S(2)}) collective-permute-start(bf16[1,4096]{1,0:T(2,128)(2,1)S(1)} %collective-permute-done.6), channel_id=1, source_target_pairs={{0,1},{1,2},{2,3},{3,4},{4,5},{5,6},{6,7},{7,8},{8,9},{9,10},{10,1... | collective-permute-start | bytes 24584 | tf_op jit(solution)/shard_map/ppermute | solution.py:68
  60.4 18.2 %collective-permute-start.8 = (bf16[1,4096]{1,0:T(2,128)(2,1)S(1)}, bf16[1,4096]{1,0:T(2,128)(2,1)S(1)}, u32[]{:S(2)}, u32[]{:S(2)}) collective-permute-start(bf16[1,4096]{1,0:T(2,128)(2,1)S(1)} %collective-permute-done.7), channel_id=1, source_target_pairs={{0,1},{1,2},{2,3},{3,4},{4,5},{5,6},{6,7},{7,8},{8,9},{9,10},{10,1... | collective-permute-start | bytes 24584 | tf_op jit(solution)/shard_map/ppermute | solution.py:68
  78.6 5.9 %collective-permute-start.9 = (bf16[1,4096]{1,0:T(2,128)(2,1)S(1)}, bf16[1,4096]{1,0:T(2,128)(2,1)S(1)}, u32[]{:S(2)}, u32[]{:S(2)}) collective-permute-start(bf16[1,4096]{1,0:T(2,128)(2,1)S(1)} %collective-permute-done.8), channel_id=1, source_target_pairs={{0,1},{1,2},{2,3},{3,4},{4,5},{5,6},{6,7},{7,8},{8,9},{9,10},{10,1... | collective-permute-start | bytes 24584 | tf_op jit(solution)/shard_map/ppermute | solution.py:68
  84.5 5.9 %collective-permute-start.10 = (bf16[1,4096]{1,0:T(2,128)(2,1)S(1)}, bf16[1,4096]{1,0:T(2,128)(2,1)S(1)}, u32[]{:S(2)}, u32[]{:S(2)}) collective-permute-start(bf16[1,4096]{1,0:T(2,128)(2,1)S(1)} %collective-permute-done.9), channel_id=1, source_target_pairs={{0,1},{1,2},{2,3},{3,4},{4,5},{5,6},{6,7},{7,8},{8,9},{9,10},{10,1... | collective-permute-start | bytes 24584 | tf_op jit(solution)/shard_map/ppermute | solution.py:68
  90.3 8.5 %collective-permute-start.11 = (bf16[1,4096]{1,0:T(2,128)(2,1)S(1)}, bf16[1,4096]{1,0:T(2,128)(2,1)S(1)}, u32[]{:S(2)}, u32[]{:S(2)}) collective-permute-start(bf16[1,4096]{1,0:T(2,128)(2,1)S(1)} %collective-permute-done.10), channel_id=1, source_target_pairs={{0,1},{1,2},{2,3},{3,4},{4,5},{5,6},{6,7},{7,8},{8,9},{9,10},{10,1... | collective-permute-start | bytes 24584 | tf_op jit(solution)/shard_map/ppermute | solution.py:68
  98.8 8.1 %collective-permute-start.12 = (bf16[1,4096]{1,0:T(2,128)(2,1)S(1)}, bf16[1,4096]{1,0:T(2,128)(2,1)S(1)}, u32[]{:S(2)}, u32[]{:S(2)}) collective-permute-start(bf16[1,4096]{1,0:T(2,128)(2,1)S(1)} %collective-permute-done.11), channel_id=1, source_target_pairs={{0,1},{1,2},{2,3},{3,4},{4,5},{5,6},{6,7},{7,8},{8,9},{9,10},{10,1... | collective-permute-start | bytes 24584 | tf_op jit(solution)/shard_map/ppermute | solution.py:68
  98.8 6.8 %copy-start.2 = (u32[32]{0:T(128)S(1)}, u32[32]{0:T(128)}, u32[]{:S(2)}) copy-start(u32[32]{0:T(128)} %constant.55) | copy-start | bytes 388
  107.0 12.9 %collective-permute-start.13 = (bf16[1,4096]{1,0:T(2,128)(2,1)S(1)}, bf16[1,4096]{1,0:T(2,128)(2,1)S(1)}, u32[]{:S(2)}, u32[]{:S(2)}) collective-permute-start(bf16[1,4096]{1,0:T(2,128)(2,1)S(1)} %collective-permute-done.12), channel_id=1, source_target_pairs={{0,1},{1,2},{2,3},{3,4},{4,5},{5,6},{6,7},{7,8},{8,9},{9,10},{10,1... | collective-permute-start | bytes 24584 | tf_op jit(solution)/shard_map/ppermute | solution.py:68
  119.9 7.0 %collective-permute-start.14 = (bf16[1,4096]{1,0:T(2,128)(2,1)S(1)}, bf16[1,4096]{1,0:T(2,128)(2,1)S(1)}, u32[]{:S(2)}, u32[]{:S(2)}) collective-permute-start(bf16[1,4096]{1,0:T(2,128)(2,1)S(1)} %collective-permute-done.13), channel_id=1, source_target_pairs={{0,1},{1,2},{2,3},{3,4},{4,5},{5,6},{6,7},{7,8},{8,9},{9,10},{10,1... | collective-permute-start | bytes 24584 | tf_op jit(solution)/shard_map/ppermute | solution.py:68
  120.0 6.9 %copy-start.1 = (bf16[1,4096]{1,0:T(2,128)(2,1)S(1)}, bf16[1,4096]{1,0:T(2,128)(2,1)}, u32[]{:S(2)}) copy-start(bf16[1,4096]{1,0:T(2,128)(2,1)} %param.6) | copy-start | bytes 24580
  144.1 13.7 %all-to-all-start.2 = ((f32[16,1,32]{2,1,0:T(1,128)}), f32[16,1,32]{2,1,0:T(1,128)S(1)}, u32[]{:S(2)}, u32[]{:S(2)}) async-start(f32[16,1,32]{2,1,0:T(1,128)} %copy.55), calls=%async_computation.2 | async-start | bytes 16384 | tf_op jit(solution)/shard_map/all_to_all | solution.py:85
  157.9 12.4 %all-to-all-start = ((f32[16,1,32]{2,1,0:T(1,128)}), f32[16,1,32]{2,1,0:T(1,128)S(1)}, u32[]{:S(2)}, u32[]{:S(2)}) async-start(f32[16,1,32]{2,1,0:T(1,128)} %copy.47), calls=%async_computation | async-start | bytes 16384 | tf_op jit(solution)/shard_map/all_to_all | solution.py:79
  170.2 14.7 %all-to-all-start.1 = ((f32[16,1,4096]{2,1,0:T(1,128)}), f32[16,1,4096]{2,1,0:T(1,128)S(1)}, u32[]{:S(2)}, u32[]{:S(2)}) async-start(f32[16,1,4096]{2,1,0:T(1,128)} %bitcast.13), calls=%async_computation.1 | async-start | bytes 524288 | tf_op jit(solution)/shard_map/all_to_all | solution.py:82
